TPU v7x, 32 devices: a whole 2x2x4 slice. The times are simulated.
32 devices in a mesh: span: 4 (over y, x), heads: 8 (over z, core).
Axes of the slice: x: 2, y: 2, z: 4, core: 2. Of those that a mesh axis runs over, the one named last changes fastest.
Arguments:
- latents: bfloat16 [4, 6144, 512], P(None, ('span', 'heads')), may hold values from -6 to 6
- rotary_rows: bfloat16 [4, 6144, 64], P(None, ('span', 'heads')), may hold values from -6 to 6
- latent_gain: float32 [512], replicated, may hold values from 0.25 to 1.75
- key_up: bfloat16 [512, 16, 128], P(None, 'heads'), may hold values from -0.25 to 0.25
- value_up: bfloat16 [512, 16, 128], P(None, 'heads'), may hold values from -0.25 to 0.25
Outputs:
- stored_keys: bfloat16 [4, 6144, 16, 192], P('span', None, 'heads')
- stored_values: bfloat16 [4, 6144, 16, 128], P('span', None, 'heads')
All inputs are finite; a program needn't handle non-finite values.
Results may differ from a plain program's by a relative error of at most 0.001.
Values may be sent and summed in bfloat16 or wider, within the bound.
A program may use at most 128 MiB of HBM per device.

v0:
```python
import jax
import jax.numpy as jnp
from jax import lax
from jax.sharding import PartitionSpec as P


def expand_rows(rows, rotary, key_up, value_up):
    wide_keys = jnp.einsum(
        "btr,rhk->bthk", rows, key_up, preferred_element_type=jnp.float32
    ).astype(jnp.bfloat16)
    shared = jnp.broadcast_to(rotary[:, :, None], wide_keys.shape[:3] + rotary.shape[2:])
    wide_values = jnp.einsum(
        "btr,rhk->bthk", rows, value_up, preferred_element_type=jnp.float32
    ).astype(jnp.bfloat16)
    return (jnp.concatenate([wide_keys, shared], axis=-1), wide_values)


def root_norm(vectors, row_gain):
    return (
        vectors * lax.rsqrt(jnp.mean(vectors * vectors, axis=-1, keepdims=True) + 1e-06) * row_gain
    )


def per_device(latents, rotary_rows, latent_gain, key_up, value_up):
    rows_ready = root_norm(latents.astype(jnp.float32), latent_gain).astype(jnp.bfloat16)
    rows_moved, rotary_moved = (
        lax.all_to_all(rows_ready, "span", split_axis=0, concat_axis=1, tiled=True),
        lax.all_to_all(rotary_rows, "span", split_axis=0, concat_axis=1, tiled=True),
    )
    rows_cut = rows_moved.reshape(
        rows_moved.shape[0], lax.axis_size("span"), -1, rows_moved.shape[2]
    )
    rotary_cut = rotary_moved.reshape(
        rotary_moved.shape[0], lax.axis_size("span"), -1, rotary_moved.shape[2]
    )
    rows_joined, rotary_joined = (
        lax.all_gather(rows_cut, "heads", axis=2, tiled=True),
        lax.all_gather(rotary_cut, "heads", axis=2, tiled=True),
    )
    rows_whole = rows_joined.reshape(rows_joined.shape[0], -1, rows_joined.shape[3])
    rotary_whole = rotary_joined.reshape(rotary_joined.shape[0], -1, rotary_joined.shape[3])
    stored_keys, stored_values = expand_rows(rows_whole, rotary_whole, key_up, value_up)
    return (stored_keys, stored_values)


def solution(mesh):
    in_specs = (
        P(None, ("span", "heads"), None),
        P(None, ("span", "heads"), None),
        P(),
        P(None, "heads", None),
        P(None, "heads", None),
    )
    out_specs = (P("span", None, "heads", None), P("span", None, "heads", None))
    return jax.shard_map(
        per_device, mesh=mesh, in_specs=in_specs, out_specs=out_specs, check_vma=False
    )
```

profile of v0, /device:TPU:0, one launch (start us, length us, event | category | flops | bytes accessed | tf_op | source)
XLA Modules:
  0.0 149.0 jit_solution(12033314378571793330)
XLA Ops:
  7.2 0.0 copy-start
  7.2 0.0 copy-start.2
  7.2 0.0 all-gather.4.cloned.1.call-start
  7.2 1.4 fusion.1
  8.7 1.4 fusion.3
  10.1 16.4 %all_to_all.8 = bf16[4,192,512]{2,1,0:T(8,128)(2,1)} all-to-all(bf16[4,192,512]{2,1,0:T(8,128)(2,1)S(1)} %fusion.3), channel_id=1, replica_groups=mesh['span'=4,'heads'=8] {'span'}, dimensions={0} | all-to-all | bytes 1572864 | tf_op jit(solution)/shard_map/all_to_all | solution.py:27
  26.5 0.0 all-gather.4.cloned.1.call-update
  26.5 3.3 %all-to-all-start.1 = ((bf16[4,192,64]{1,2,0:T(8,128)(2,1)}), bf16[4,192,64]{1,2,0:T(8,128)(2,1)S(1)}, u32[]{:S(2)}, u32[]{:S(2)}) async-start(bf16[4,192,64]{1,2,0:T(8,128)(2,1)} %param.6), calls=%async_computation.1 | async-start | bytes 262144 | tf_op jit(solution)/shard_map/all_to_all | solution.py:28
  29.9 0.0 copy-done.2
  29.9 0.2 copy.19
  30.1 4.8 %all-to-all-done.1 = bf16[4,192,64]{1,2,0:T(8,128)(2,1)S(1)} async-done(((bf16[4,192,64]{1,2,0:T(8,128)(2,1)}), bf16[4,192,64]{1,2,0:T(8,128)(2,1)S(1)}, u32[]{:S(2)}, u32[]{:S(2)}) %all-to-all-start.1) | async-done | bytes 98336 | tf_op jit(solution)/shard_map/all_to_all | solution.py:28
  34.9 0.2 copy.20
  35.0 31.3 %all-gather.1 = bf16[4,1536,64]{2,0,1:T(4,128)(2,1)S(1)} all-gather(bf16[4,192,64]{2,0,1:T(4,128)(2,1)S(1)} %copy.20), channel_id=3, replica_groups=mesh['span'=4,'heads'=8] {'heads'}, dimensions={1}, use_global_device_ids=true | all-gather | bytes 884736 | tf_op jit(solution)/shard_map/all_gather | solution.py:38
  66.4 1.2 copy.21
  67.5 0.1 copy.24
  67.7 35.9 %all-gather.4.cloned.1.call-done = bf16[4,1536,512]{2,1,0:T(8,128)(2,1)} async-done(((bf16[4,192,512]{2,1,0:T(8,128)(2,1)}), bf16[4,1536,512]{2,1,0:T(8,128)(2,1)}) %all-gather.4.cloned.1.call-update) | async-done | bytes 6291472 | tf_op jit(solution)/shard_map/all_gather | solution.py:37
  103.6 4.6 %fusion.5 = f32[6144,256]{0,1:S(1)} fusion(bf16[6144,512]{1,0:T(8,128)(2,1)} %bitcast.17, bf16[512,256]{0,1:T(8,128)(2,1)S(1)} %bitcast.21), kind=kOutput, calls=%fused_computation.11 | convolution fusion | flops 1610612736 | bytes 12845056
  108.2 0.0 copy-start.1
  108.2 0.4 convert_bitcast_fusion
  108.6 0.0 copy-done
  108.6 2.3 %copy-done.1 = bf16[4,1536,512]{2,1,0:T(8,128)(2,1)S(1)} copy-done((bf16[4,1536,512]{2,1,0:T(8,128)(2,1)S(1)}, bf16[4,1536,512]{2,1,0:T(8,128)(2,1)}, u32[]{:S(2)}) %copy-start.1) | copy-done | bytes 6291480
  111.0 1.8 %fusion = bf16[1,6144,2,128]{3,1,2,0:T(8,128)(2,1)S(1)} fusion(bf16[6144,512,1]{1,0,2:T(8,128)(2,1)S(1)} %bitcast.18, bf16[512,2,128]{2,1,0:T(2,128)(2,1)S(1)} %copy-done), kind=kOutput, calls=%fused_computation.1 | convolution fusion | flops 1612185600 | bytes 9699328 | tf_op jit(solution)/shard_map/btr,rhk->bthk/dot_general | solution.py:12
  112.8 26.8 %copy.23 = bf16[1,6144,2,128]{3,2,1,0:T(2,128)(2,1)} copy(bf16[1,6144,2,128]{3,1,2,0:T(8,128)(2,1)S(1)} %fusion) | data formatting | bytes 6291456
  139.5 0.1 broadcast_in_dim.10
  139.7 2.5 %pad_maximum_fusion = bf16[1,6144,2,192]{1,3,2,0:T(8,128)(2,1)} fusion(bf16[1,6144,2,64]{1,3,2,0:T(8,128)(2,1)S(1)} %broadcast_in_dim.10, bf16[1,6144,2,128]{1,3,2,0:T(8,128)(2,1)S(1)} %convert_bitcast_fusion), kind=kLoop, calls=%fused_computation.2 | loop fusion | flops 9437184 | bytes 9437184 | tf_op jit(solution)/shard_map/concatenate | solution.py:15
  (1 shorter events, 0.0 us)
Async XLA Ops:
  7.2 101.5 %copy-start = (bf16[512,2,128]{2,1,0:T(2,128)(2,1)S(1)}, bf16[512,2,128]{2,1,0:T(2,128)(2,1)}, u32[]{:S(2)}) copy-start(bf16[512,2,128]{2,1,0:T(2,128)(2,1)} %param.9) | copy-start | bytes 786436
  7.2 22.7 %copy-start.2 = (bf16[512,2,128]{2,1,0:T(2,128)(2,1)S(1)}, bf16[512,2,128]{2,1,0:T(2,128)(2,1)}, u32[]{:S(2)}) copy-start(bf16[512,2,128]{2,1,0:T(2,128)(2,1)} %param.8) | copy-start | bytes 786436
  7.2 96.4 %all-gather.4.cloned.1.call-start = ((), (), s32[]{:S(2)}) async-start(), calls=%async_computation.2 | async-start | bytes 7077888 | tf_op jit(solution)/shard_map/all_gather | solution.py:37
  26.5 8.3 %all-to-all-start.1 = ((bf16[4,192,64]{1,2,0:T(8,128)(2,1)}), bf16[4,192,64]{1,2,0:T(8,128)(2,1)S(1)}, u32[]{:S(2)}, u32[]{:S(2)}) async-start(bf16[4,192,64]{1,2,0:T(8,128)(2,1)} %param.6), calls=%async_computation.1 | async-start | bytes 262144 | tf_op jit(solution)/shard_map/all_to_all | solution.py:28
  108.2 2.8 %copy-start.1 = (bf16[4,1536,512]{2,1,0:T(8,128)(2,1)S(1)}, bf16[4,1536,512]{2,1,0:T(8,128)(2,1)}, u32[]{:S(2)}) copy-start(bf16[4,1536,512]{2,1,0:T(8,128)(2,1)} %all-gather.4.cloned.1.call-done) | copy-start | bytes 18874372
Sparse Core Ops, SparseCore 0:
  26.6 76.8 all-gather.3
where the time goes:
time: 149 us
  blocking collectives  47.8 us (32%)
  waiting for transfers between devices  40.7 us (27%)
  local copies, waits for them, and re-layouts  30.9 us (21%)
  between operations  14.2 us (10%)
  matrix products  6.4 us (4%)
  other arithmetic  5.74 us (4%)
  starting transfers between devices  3.38 us (2%)
    all_gather x1, waiting for transfers between devices, per_device(): lax.all_gather(rows_cut, 'heads', axis=2, tiled=True)  35.9 us
    all_gather x1, blocking collectives, per_device(): lax.all_gather(rotary_cut, 'heads', axis=2, tiled=True)  31.3 us
    unnamed x9, local copies, waits for them, and re-layouts  29.4 us
    all_to_all x1, blocking collectives, per_device(): lax.all_to_all(rows_ready, 'span', split_axis=0, concat_axis=1, tiled=True)  16.4 us
    all_to_all x1, waiting for transfers between devices, per_device(): lax.all_to_all(rotary_rows, 'span', split_axis=0, concat_axis=1, tiled=True)  4.81 us
    unnamed x1, matrix products  4.61 us
    all_to_all x1, starting transfers between devices, per_device(): lax.all_to_all(rotary_rows, 'span', split_axis=0, concat_axis=1, tiled=True)  3.34 us
  transfers between devices with their start and end apart: 2, of which 2 were waited for; matrix products, arithmetic and copies ran while one was open for 1% of the time, Pallas kernels for 0%

commit v1 on v0

--- a/solution.py
+++ b/solution.py
@@ -2,6 +2,12 @@
 import jax.numpy as jnp
 from jax import lax
 from jax.sharding import PartitionSpec as P
+
+
+def exchange_blocks(block, axis, split, join):
+    parts = jnp.split(block, lax.axis_size(axis), axis=split)
+    incoming = lax.all_to_all(jnp.stack(parts), axis, 0, 0)
+    return jnp.concatenate(incoming, axis=join)
 
 
 def expand_rows(rows, rotary, key_up, value_up):
@@ -25,7 +31,7 @@
     rows_ready = root_norm(latents.astype(jnp.float32), latent_gain).astype(jnp.bfloat16)
     rows_moved, rotary_moved = (
         lax.all_to_all(rows_ready, "span", split_axis=0, concat_axis=1, tiled=True),
-        lax.all_to_all(rotary_rows, "span", split_axis=0, concat_axis=1, tiled=True),
+        exchange_blocks(rotary_rows, "span", 0, 1),
     )
     rows_cut = rows_moved.reshape(
         rows_moved.shape[0], lax.axis_size("span"), -1, rows_moved.shape[2]

time: 149 us -> 149 us (level)
    unnamed x9 -> x11, local copies, waits for them, and re-layouts: 29.4 us -> 29.4 us
  transfers between devices with their start and end apart: 2 -> 2, of which waited for: 2 -> 2; matrix products, arithmetic and copies ran while one was open for 1% -> 2% of each run, Pallas kernels for 0% -> 0%
where the time goes in v1:
time: 149 us
  blocking collectives  47.8 us (32%)
  waiting for transfers between devices  40 us (27%)
  local copies, waits for them, and re-layouts  30.9 us (21%)
  between operations  14.2 us (10%)
  other arithmetic  6.43 us (4%)
  matrix products  6.41 us (4%)
  starting transfers between devices  3.36 us (2%)
    all_gather x1, waiting for transfers between devices, per_device(): lax.all_gather(rows_cut, 'heads', axis=2, tiled=True)  35.2 us
    all_gather x1, blocking collectives, per_device(): lax.all_gather(rotary_cut, 'heads', axis=2, tiled=True)  31.3 us
    unnamed x11, local copies, waits for them, and re-layouts  29.4 us
    all_to_all x1, blocking collectives, per_device(): lax.all_to_all(rows_ready, 'span', split_axis=0, concat_axis=1, tiled=True)  16.4 us
    all_to_all x1, waiting for transfers between devices, exchange_blocks(): incoming = lax.all_to_all(jnp.stack(parts), axis, 0, 0)  4.81 us
    unnamed x1, matrix products  4.61 us
    all_to_all x1, starting transfers between devices, exchange_blocks(): incoming = lax.all_to_all(jnp.stack(parts), axis, 0, 0)  3.33 us
  transfers between devices with their start and end apart: 2, of which 2 were waited for; matrix products, arithmetic and copies ran while one was open for 2% of the time, Pallas kernels for 0%

profile of v1, /device:TPU:0, one launch (start us, length us, event | category | flops | bytes accessed | tf_op | source)
XLA Modules:
  0.0 149.0 jit_solution(16935356483599078159)
XLA Ops:
  7.2 0.0 copy-start
  7.2 0.0 copy-start.3
  7.2 0.0 copy-start.2
  7.2 0.0 all-gather.4.cloned.1.call-start
  7.2 1.4 fusion.1
  8.7 1.4 fusion.3
  10.1 16.4 %all_to_all.14 = bf16[4,192,512]{2,1,0:T(8,128)(2,1)} all-to-all(bf16[4,192,512]{2,1,0:T(8,128)(2,1)S(1)} %fusion.3), channel_id=1, replica_groups=mesh['span'=4,'heads'=8] {'span'}, dimensions={0} | all-to-all | bytes 1572864 | tf_op jit(solution)/shard_map/all_to_all | solution.py:33
  26.5 0.0 all-gather.4.cloned.1.call-update
  26.5 0.0 copy-done.3
  26.6 0.7 pad_maximum_fusion.1
  27.3 3.3 %all-to-all-start.1 = ((bf16[4,1,192,64]{2,3,1,0:T(8,128)(2,1)}), bf16[4,1,192,64]{2,3,1,0:T(8,128)(2,1)S(1)}, u32[]{:S(2)}, u32[]{:S(2)}) async-start(bf16[4,1,192,64]{2,3,1,0:T(8,128)(2,1)} %pad_maximum_fusion.1), calls=%async_computation.1 | async-start | bytes 262144 | tf_op jit(solution)/shard_map/all_to_all | solution.py:9
  30.6 0.0 copy-done.2
  30.6 0.2 copy.22
  30.8 4.8 %all-to-all-done.1 = bf16[4,1,192,64]{2,3,1,0:T(8,128)(2,1)S(1)} async-done(((bf16[4,1,192,64]{2,3,1,0:T(8,128)(2,1)}), bf16[4,1,192,64]{2,3,1,0:T(8,128)(2,1)S(1)}, u32[]{:S(2)}, u32[]{:S(2)}) %all-to-all-start.1) | async-done | bytes 98336 | tf_op jit(solution)/shard_map/all_to_all | solution.py:9
  35.6 0.2 copy.23
  35.7 31.3 %all-gather.1 = bf16[4,1,1536,64]{3,0,1,2:T(4,128)(2,1)S(1)} all-gather(bf16[4,1,192,64]{3,0,1,2:T(4,128)(2,1)S(1)} %copy.23), channel_id=3, replica_groups=mesh['span'=4,'heads'=8] {'heads'}, dimensions={2}, use_global_device_ids=true | all-gather | bytes 884736 | tf_op jit(solution)/shard_map/all_gather | solution.py:44
  67.1 1.2 copy.24
  68.3 0.1 copy.27
  68.4 35.2 %all-gather.4.cloned.1.call-done = bf16[4,1536,512]{2,1,0:T(8,128)(2,1)} async-done(((bf16[4,192,512]{2,1,0:T(8,128)(2,1)}), bf16[4,1536,512]{2,1,0:T(8,128)(2,1)}) %all-gather.4.cloned.1.call-update) | async-done | bytes 6291472 | tf_op jit(solution)/shard_map/all_gather | solution.py:43
  103.6 4.6 %fusion.5 = f32[6144,256]{0,1:S(1)} fusion(bf16[6144,512]{1,0:T(8,128)(2,1)} %bitcast.26, bf16[512,256]{0,1:T(8,128)(2,1)S(1)} %bitcast.30), kind=kOutput, calls=%fused_computation.16 | convolution fusion | flops 1610612736 | bytes 12845056
  108.2 0.0 copy-start.1
  108.2 0.4 convert_bitcast_fusion
  108.6 0.0 copy-done
  108.6 2.3 %copy-done.1 = bf16[4,1536,512]{2,1,0:T(8,128)(2,1)S(1)} copy-done((bf16[4,1536,512]{2,1,0:T(8,128)(2,1)S(1)}, bf16[4,1536,512]{2,1,0:T(8,128)(2,1)}, u32[]{:S(2)}) %copy-start.1) | copy-done | bytes 6291480
  111.0 1.8 %fusion = bf16[1,6144,2,128]{3,1,2,0:T(8,128)(2,1)S(1)} fusion(bf16[6144,512,1]{1,0,2:T(8,128)(2,1)S(1)} %bitcast.27, bf16[512,2,128]{2,1,0:T(2,128)(2,1)S(1)} %copy-done), kind=kOutput, calls=%fused_computation.1 | convolution fusion | flops 1612185600 | bytes 9699328 | tf_op jit(solution)/shard_map/btr,rhk->bthk/dot_general | solution.py:18
  112.8 26.8 %copy.26 = bf16[1,6144,2,128]{3,2,1,0:T(2,128)(2,1)} copy(bf16[1,6144,2,128]{3,1,2,0:T(8,128)(2,1)S(1)} %fusion) | data formatting | bytes 6291456
  139.5 0.1 broadcast_in_dim.10
  139.7 2.5 %pad_maximum_fusion = bf16[1,6144,2,192]{1,3,2,0:T(8,128)(2,1)} fusion(bf16[1,6144,2,64]{1,3,2,0:T(8,128)(2,1)S(1)} %broadcast_in_dim.10, bf16[1,6144,2,128]{1,3,2,0:T(8,128)(2,1)S(1)} %convert_bitcast_fusion), kind=kLoop, calls=%fused_computation.2 | loop fusion | flops 9437184 | bytes 9437184 | tf_op jit(solution)/shard_map/concatenate | solution.py:21
  (2 shorter events, 0.0 us)
Async XLA Ops:
  7.2 101.5 %copy-start = (bf16[512,2,128]{2,1,0:T(2,128)(2,1)S(1)}, bf16[512,2,128]{2,1,0:T(2,128)(2,1)}, u32[]{:S(2)}) copy-start(bf16[512,2,128]{2,1,0:T(2,128)(2,1)} %param.9) | copy-start | bytes 786436
  7.2 19.4 %copy-start.3 = (bf16[4,192,64]{1,2,0:T(8,128)(2,1)S(1)}, bf16[4,192,64]{1,2,0:T(8,128)(2,1)}, u32[]{:S(2)}) copy-start(bf16[4,192,64]{1,2,0:T(8,128)(2,1)} %param.6) | copy-start | bytes 294916
  7.2 23.4 %copy-start.2 = (bf16[512,2,128]{2,1,0:T(2,128)(2,1)S(1)}, bf16[512,2,128]{2,1,0:T(2,128)(2,1)}, u32[]{:S(2)}) copy-start(bf16[512,2,128]{2,1,0:T(2,128)(2,1)} %param.8) | copy-start | bytes 786436
  7.2 96.4 %all-gather.4.cloned.1.call-start = ((), (), s32[]{:S(2)}) async-start(), calls=%async_computation.2 | async-start | bytes 7077888 | tf_op jit(solution)/shard_map/all_gather | solution.py:43
  27.3 8.3 %all-to-all-start.1 = ((bf16[4,1,192,64]{2,3,1,0:T(8,128)(2,1)}), bf16[4,1,192,64]{2,3,1,0:T(8,128)(2,1)S(1)}, u32[]{:S(2)}, u32[]{:S(2)}) async-start(bf16[4,1,192,64]{2,3,1,0:T(8,128)(2,1)} %pad_maximum_fusion.1), calls=%async_computation.1 | async-start | bytes 262144 | tf_op jit(solution)/shard_map/all_to_all | solution.py:9
  108.2 2.8 %copy-start.1 = (bf16[4,1536,512]{2,1,0:T(8,128)(2,1)S(1)}, bf16[4,1536,512]{2,1,0:T(8,128)(2,1)}, u32[]{:S(2)}) copy-start(bf16[4,1536,512]{2,1,0:T(8,128)(2,1)} %all-gather.4.cloned.1.call-done) | copy-start | bytes 18874372
Sparse Core Ops, SparseCore 0:
  26.7 76.8 all-gather.3
